TPU v7x, 32 devices: a whole 2x2x4 slice. The times are simulated.
32 devices in a mesh: dp: 8 (over z, x), mp: 4 (over y, core).
Axes of the slice: x: 2, y: 2, z: 4, core: 2. Of those that a mesh axis runs over, the one named last changes fastest.
Arguments:
- patches: bfloat16 [4096, 2048], P('dp'), may hold values from -6 to 6
- cotangent: bfloat16 [4096, 8192], P('dp', 'mp'), may hold values from -0.09375 to 0.09375
- weight: float32 [2048, 8192], P('dp', 'mp'), may hold values from -0.125 to 0.125
- accum: float32 [2048, 8192], P('dp', 'mp'), may hold values from 0.1 to 4
Outputs:
- new_weight: float32 [2048, 8192], P(('dp', 'mp'))
- new_accum: float32 [2048, 8192], P(('dp', 'mp'))
- weight_copy: bfloat16 [2048, 8192], P(None, 'mp')
All inputs are finite; a program needn't handle non-finite values.
Results may differ from a plain program's by a relative error of at most 0.001.
Values may be sent and summed in bfloat16 or wider, within the bound.
A program may use at most 192 MiB of HBM per device.

v0:
```python
import jax
import jax.numpy as jnp
from jax import lax
from jax.sharding import PartitionSpec as P

learning_rate = 0.02


def adagrad(accum, weight, grad):
    summed = accum + grad * grad
    return (summed, weight - learning_rate * grad * lax.rsqrt(summed))


def shards(patches, cotangent, weight, accum):
    patch_block = lax.all_to_all(patches, "dp", split_axis=1, concat_axis=0, tiled=True)
    grad_block = jnp.einsum(
        "tr,tf->rf",
        patch_block,
        lax.all_gather(cotangent, "dp", axis=0, tiled=True),
        preferred_element_type=jnp.float32,
    )
    accum_block, weight_block = adagrad(accum, weight, grad_block)
    weight_copy = lax.all_gather(weight_block.astype(jnp.bfloat16), "dp", axis=0, tiled=True)
    new_accum, new_weight = (
        lax.all_to_all(accum_block, "mp", split_axis=0, concat_axis=1, tiled=True),
        lax.all_to_all(weight_block, "mp", split_axis=0, concat_axis=1, tiled=True),
    )
    return (new_weight, new_accum, weight_copy)


def solution(mesh):
    return jax.shard_map(
        shards,
        mesh=mesh,
        in_specs=(P("dp", None), P("dp", "mp"), P("dp", "mp"), P("dp", "mp")),
        out_specs=(P(("dp", "mp"), None), P(("dp", "mp"), None), P(None, "mp")),
        check_vma=False,
    )
```

profile of v0, /device:TPU:0, one launch (start us, length us, event | category | flops | bytes accessed | tf_op | source)
XLA Modules:
  0.0 430.2 jit_solution(2336489553796141500)
XLA Ops:
  7.2 0.0 all-gather.3.cloned.1.call-start
  7.2 0.7 all-gather.3.cloned.1.call-update
  7.9 0.0 all-gather.5.cloned.1.call-start
  7.9 2.9 copy.11
  10.8 107.2 %all_to_all.57 = bf16[512,8,256]{0,2,1:T(8,128)(2,1)} all-to-all(bf16[512,8,256]{0,2,1:T(8,128)(2,1)S(1)} %bitcast.18), channel_id=1, replica_groups=mesh['dp'=8,'mp'=4] {'dp'}, dimensions={1} | all-to-all | bytes 4194304 | tf_op jit(solution)/shard_map/all_to_all | solution.py:15
  118.0 2.8 copy.12
  120.9 158.3 %all-gather.3.cloned.1.call-done = bf16[4096,2048]{1,0:T(8,128)(2,1)} async-done(((bf16[512,2048]{1,0:T(8,128)(2,1)}), bf16[4096,2048]{1,0:T(8,128)(2,1)}) %all-gather.3.cloned.1.call-update) | async-done | bytes 16777232 | tf_op jit(solution)/shard_map/all_gather | solution.py:19
  279.1 12.9 %fusion = (bf16[256,2048]{1,0:T(8,128)(2,1)}, f32[256,2048]{1,0:T(8,128)}, f32[256,2048]{1,0:T(8,128)}) fusion(f32[256,2048]{1,0:T(8,128)} %param.6, f32[256,2048]{1,0:T(8,128)} %param.7, bf16[4096,256]{1,0:T(8,128)(2,1)S(1)} %bitcast.13, bf16[4096,2048]{1,0:T(8,128)(2,1)} %all-gather.3.cloned.1.call-done), kind=kOutput, calls=%fused_computation.2 | convolution fusion | flops 4298113024 | bytes 28311552 | tf_op jit(solution)/shard_map/tr,tf->rf/dot_general | solution.py:16
  292.0 0.0 all-gather.5.cloned.1.call-update
  292.1 30.2 %all_to_all.58 = f32[4,64,2048]{2,1,0:T(8,128)} all-to-all(f32[4,64,2048]{2,1,0:T(8,128)} %bitcast.14), channel_id=1, replica_groups=mesh['dp'=8,'mp'=4] {'mp'}, dimensions={0} | all-to-all | bytes 4194304 | tf_op jit(solution)/shard_map/all_to_all | solution.py:26
  322.2 3.6 all-to-all-start.2
  325.8 3.1 copy.15
  329.0 22.5 %all-to-all-done.2 = f32[4,64,2048]{2,1,0:T(8,128)S(1)} async-done(((f32[4,64,2048]{2,1,0:T(8,128)}), f32[4,64,2048]{2,1,0:T(8,128)S(1)}, u32[]{:S(2)}, u32[]{:S(2)}) %all-to-all-start.2) | async-done | bytes 2097184 | tf_op jit(solution)/shard_map/all_to_all | solution.py:25
  351.5 1.5 copy.16
  352.9 61.9 %all-gather.5.cloned.1.call-done = bf16[2048,2048]{1,0:T(8,128)(2,1)} async-done(((bf16[256,2048]{1,0:T(8,128)(2,1)}), bf16[2048,2048]{1,0:T(8,128)(2,1)}) %all-gather.5.cloned.1.call-update) | async-done | bytes 8388624 | tf_op jit(solution)/shard_map/all_gather | solution.py:23
  414.9 8.4 %copy.18 = bf16[2048,2048]{1,0:T(8,128)(2,1)} copy(bf16[2048,2048]{1,0:T(8,128)(2,1)} %all-gather.5.cloned.1.call-done) | data formatting | bytes 16777216
Async XLA Ops:
  7.2 272.0 %all-gather.3.cloned.1.call-start = ((), (), s32[]{:S(2)}) async-start(), calls=%async_computation.3 | async-start | bytes 18874368 | tf_op jit(solution)/shard_map/all_gather | solution.py:19
  7.9 407.0 %all-gather.5.cloned.1.call-start = ((), (), s32[]{:S(2)}) async-start(), calls=%async_computation.4 | async-start | bytes 9437184 | tf_op jit(solution)/shard_map/all_gather | solution.py:23
  322.2 29.3 %all-to-all-start.2 = ((f32[4,64,2048]{2,1,0:T(8,128)}), f32[4,64,2048]{2,1,0:T(8,128)S(1)}, u32[]{:S(2)}, u32[]{:S(2)}) async-start(f32[4,64,2048]{2,1,0:T(8,128)} %bitcast.5), calls=%async_computation.2 | async-start | bytes 4194304 | tf_op jit(solution)/shard_map/all_to_all | solution.py:25
Sparse Core Ops, SparseCore 0:
  10.1 268.9 all-gather.2
  292.2 122.6 all-gather.4
where the time goes:
time: 431 us; the launch traced here: 430 us
  waiting for transfers between devices  243 us (56%)
  blocking collectives  137 us (32%)
  local copies, waits for them, and re-layouts  18.8 us (4%)
  between operations  14.1 us (3%)
  matrix products  12.9 us (3%)
    all_gather x1, waiting for transfers between devices, shards(): lax.all_gather(cotangent, 'dp', axis=0, tiled=True)  158 us
    all_to_all x1, blocking collectives, shards(): lax.all_to_all(patches, 'dp', split_axis=1, concat_axis=0, tiled=True)  107 us
    all_gather x1, waiting for transfers between devices, shards(): lax.all_gather(weight_block.astype(jnp.bfloat16), 'dp', axis=0, tiled=True)  61.9 us
    all_to_all x1, blocking collectives, shards(): lax.all_to_all(weight_block, 'mp', split_axis=0, concat_axis=1, tiled=True)  30.2 us
    all_to_all x1, waiting for transfers between devices, shards(): lax.all_to_all(accum_block, 'mp', split_axis=0, concat_axis=1, tiled=True)  22.5 us
    dot_general x1, matrix products, shards(): jnp.einsum('tr,tf->rf', patch_block, lax.all_gather(cotangent, 'dp', axis...  12.9 us
    unnamed x2, local copies, waits for them, and re-layouts  11.3 us
  transfers between devices with their start and end apart: 3, of which 3 were waited for; matrix products, arithmetic and copies ran while one was open for 2% of the time, Pallas kernels for 0%

commit v1 on v0

v1 whole, which is shorter than its diff:
```python
import functools

import jax
import jax.numpy as jnp
from jax import lax
from jax.experimental import pallas as pl
from jax.experimental.pallas import tpu as pltpu
from jax.sharding import PartitionSpec as P

learning_rate = 0.02
chunks = 8


def kernel(a, b, m, p_ref, t_ref, w_ref, s_ref, ow_ref, os_ref, oc_ref,
           pv, tv, wv, sv, cv, rbuf, sbuf,
           psem, tsem, lsem, rsend, rrecv, csend, crecv, xsend, xrecv, msend, mrecv, osem):
    nc, _, tok, cc = tv.shape
    rows, full = w_ref.shape
    sub = rows // m
    me = lax.axis_index("dp")
    mi = lax.axis_index("mp")
    zi = lax.div(me, b)
    xi = lax.rem(me, b)
    has_left = zi > 0
    has_right = zi < a - 1

    def inner(j):
        return lax.rem(xi + j, b)

    def peer(j):
        return {"dp": zi * b + inner(j)}

    def other(j):
        return lax.rem(mi + j, m)

    left, right = {"dp": me - b}, {"dp": me + b}

    def remote(src, dst, send, recv, device):
        return pltpu.make_async_remote_copy(
            src_ref=src, dst_ref=dst, send_sem=send, recv_sem=recv,
            device_id=device, device_id_type=pl.DeviceIdType.MESH)

    def cols(c):
        return pl.ds(pl.multiple_of(c * cc, cc), cc)

    def block(i):
        return pl.ds(pl.multiple_of(i * rows, rows), rows)

    def own_tokens(c):
        return pltpu.make_async_copy(t_ref.at[:, cols(c)], tv.at[c, xi], lsem.at[0, c])

    def own_weight(c):
        return pltpu.make_async_copy(w_ref.at[:, cols(c)], wv.at[c], lsem.at[1, c])

    def own_accum(c):
        return pltpu.make_async_copy(s_ref.at[:, cols(c)], sv.at[c], lsem.at[2, c])

    def own_features(d):
        return pltpu.make_async_copy(p_ref.at[block(d * b + xi)], pv.at[d, xi], psem.at[2, d, 0])

    def send_tokens(c, j):
        return remote(t_ref.at[:, cols(c)], tv.at[c, xi], tsem.at[0, c, j], tsem.at[1, c, j], peer(j))

    def recv_tokens(c, j):
        return remote(t_ref.at[:, cols(c)], tv.at[c, inner(b - j)], tsem.at[0, c, j], tsem.at[1, c, j], peer(j))

    def send_features(d, j):
        return remote(p_ref.at[block(d * b + inner(j))], pv.at[d, xi], psem.at[0, d, j], psem.at[1, d, j], peer(j))

    def recv_features(d, j):
        return remote(p_ref.at[block(d * b + xi)], pv.at[d, inner(b - j)], psem.at[0, d, j], psem.at[1, d, j], peer(j))

    def pass_sum(side, c, d):
        return remote(sbuf.at[c, d], rbuf.at[side, c, d], rsend.at[c, d], rrecv.at[side, c, d],
                      right if side == 0 else left)

    def region(owner, c):
        return oc_ref.at[block(owner), cols(c)]

    def pass_copy(side, c, h, owner, src=None):
        return remote(region(owner, c) if src is None else src, region(owner, c),
                      csend.at[side, c, h], crecv.at[side, c, h], right if side == 0 else left)

    def share_copy(c, z, j, src=None):
        owner = z * b + xi
        return remote(region(owner, c) if src is None else src, region(owner, c),
                      xsend.at[c, z, j], xrecv.at[c, z, j], peer(j))

    def recv_share(c, z, j):
        spot = region(z * b + inner(b - j), c)
        return remote(spot, spot, xsend.at[c, z, j], xrecv.at[c, z, j], peer(j))

    def flat(c, k, src_dev):
        ref = ow_ref if k == 0 else os_ref
        start = pl.multiple_of(src_dev * full + c * cc, cc)
        return ref.at[:, pl.ds(start, cc)]

    def part(c, k, i):
        v = wv if k == 0 else sv
        return v.at[c, pl.ds(pl.multiple_of(i * sub, sub), sub)]

    def send_flat(c, k, j):
        return remote(part(c, k, other(j)), flat(c, k, mi), msend.at[c, k, j], mrecv.at[c, k, j], {"mp": other(j)})

    def recv_flat(c, k, j):
        return remote(part(c, k, mi), flat(c, k, other(m - j)), msend.at[c, k, j], mrecv.at[c, k, j], {"mp": other(j)})

    def own_flat(c, k):
        return pltpu.make_async_copy(part(c, k, mi), flat(c, k, mi), osem.at[c, k])

    def own_copy(c):
        return pltpu.make_async_copy(cv.at[c], region(me, c), osem.at[c, 2])

    barrier = pltpu.get_barrier_semaphore()

    def greet(device):
        pl.semaphore_signal(barrier, inc=1, device_id=device, device_id_type=pl.DeviceIdType.MESH)

    for d in range(a):
        own_features(d).start()

    @pl.loop(0, nc)
    def _(c):
        own_tokens(c).start()
        own_weight(c).start()
        own_accum(c).start()

    for j in range(1, b):
        greet(peer(j))
    for j in range(1, m):
        greet({"mp": other(j)})
    pl.when(has_left)(lambda: greet(left))
    pl.when(has_right)(lambda: greet(right))
    pl.semaphore_wait(barrier, b - 1 + m - 1 + jnp.minimum(zi, 1) + jnp.minimum(a - 1 - zi, 1))

    for j in range(1, b):
        send_tokens(0, j).start()
    order = []
    for k in range(a):
        for d in (a - 1 - k, k):
            if d not in order:
                order.append(d)
    for d in order:
        for j in range(1, b):
            send_features(d, j).start()

    @pl.loop(1, nc)
    def _(c):
        for j in range(1, b):
            send_tokens(c, j).start()

    def partial(c, d):
        total = jnp.dot(pv[d, 0], tv[c, 0], preferred_element_type=jnp.float32)
        for x in range(1, b):
            total += jnp.dot(pv[d, x], tv[c, x], preferred_element_type=jnp.float32)
        return total

    def stage_sums(c):
        own_tokens(c).wait()
        for j in range(1, b):
            recv_tokens(c, j).wait_recv()

        @pl.when(c == 0)
        def _():
            for d in order:
                own_features(d).wait()
                for j in range(1, b):
                    recv_features(d, j).wait_recv()

        def step(side, d):
            sbuf[c, d] = partial(c, d)

            @pl.when(has_left if side == 0 else has_right)
            def _():
                pass_sum(side, c, d).wait_recv()
                sbuf[c, d] += rbuf[side, c, d]

            pass_sum(side, c, d).start()

        for k in range(a):
            pl.when(a - 1 - k > zi)(functools.partial(step, 0, a - 1 - k))
            pl.when(k < zi)(functools.partial(step, 1, k))

    def stage_update(c):
        own_weight(c).wait()
        own_accum(c).wait()
        sbuf[c, zi] = partial(c, zi)
        for side, there in ((0, has_left), (1, has_right)):
            @pl.when(there)
            def _(side=side):
                pass_sum(side, c, zi).wait_recv()
                sbuf[c, zi] += rbuf[side, c, zi]
        grad = sbuf[c, zi]
        summed = sv[c] + grad * grad
        weight = wv[c] - learning_rate * grad * lax.rsqrt(summed)
        sv[c] = summed
        wv[c] = weight
        cv[c] = weight.astype(cv.dtype)
        pl.when(has_right)(lambda: pass_copy(0, c, 0, me, cv.at[c]).start())
        pl.when(has_left)(lambda: pass_copy(1, c, 0, me, cv.at[c]).start())
        for j in range(1, b):
            share_copy(c, zi, j, cv.at[c]).start()
        own_copy(c).start()
        for k in range(2):
            for j in range(1, m):
                send_flat(c, k, j).start()
            own_flat(c, k).start()

    def stage_forward(h, c):
        def hop(side):
            owner_z = zi - h if side == 0 else zi + h
            owner = owner_z * b + xi
            pass_copy(side, c, h - 1, owner).wait_recv()
            pl.when(has_right if side == 0 else has_left)(
                lambda: pass_copy(side, c, h, owner).start())
            for j in range(1, b):
                share_copy(c, owner_z, j).start()

        pl.when(zi >= h)(functools.partial(hop, 0))
        pl.when(zi + h < a)(functools.partial(hop, 1))

    @pl.loop(0, nc + a)
    def _(i):
        pl.when(i < nc)(lambda: stage_sums(i))
        pl.when((i >= 1) & (i - 1 < nc))(lambda: stage_update(i - 1))
        for h in range(1, a):
            pl.when((i >= 1 + h) & (i - 1 - h < nc))(lambda h=h: stage_forward(h, i - 1 - h))

    for d in range(a):
        for j in range(1, b):
            send_features(d, j).wait_send()

    @pl.loop(0, nc)
    def _(c):
        for j in range(1, b):
            send_tokens(c, j).wait_send()
            for z in range(a):
                share_copy(c, z, j).wait_send()
                recv_share(c, z, j).wait_recv()
        for d in range(a):
            pl.when(d != zi)(lambda d=d: pass_sum(0, c, d).wait_send())
        for h in range(a - 1):
            pl.when((zi >= h) & has_right)(lambda h=h: pass_copy(0, c, h, me).wait_send())
            pl.when((zi + h < a) & has_left)(lambda h=h: pass_copy(1, c, h, me).wait_send())
        own_copy(c).wait()
        for k in range(2):
            for j in range(1, m):
                send_flat(c, k, j).wait_send()
                recv_flat(c, k, j).wait_recv()
            own_flat(c, k).wait()


def shards(n, m, patches, cotangent, weight, accum):
    a = 1
    while a * a < n:
        a *= 2
    b = n // a
    nc = chunks
    tok, dim = patches.shape
    rows, full = weight.shape
    cc = full // nc
    f32, bf16 = jnp.float32, jnp.bfloat16
    dma = pltpu.SemaphoreType.DMA
    flops = 2 * tok * b * a * rows * full
    return pl.pallas_call(
        functools.partial(kernel, a, b, m),
        out_shape=(
            jax.ShapeDtypeStruct((rows // m, full * m), f32),
            jax.ShapeDtypeStruct((rows // m, full * m), f32),
            jax.ShapeDtypeStruct((dim, full), bf16),
        ),
        in_specs=[pl.BlockSpec(memory_space=pl.ANY)] * 4,
        out_specs=(pl.BlockSpec(memory_space=pl.ANY),) * 3,
        scratch_shapes=[
            pltpu.VMEM((a, b, rows, tok), bf16),
            pltpu.VMEM((nc, b, tok, cc), bf16),
            pltpu.VMEM((nc, rows, cc), f32),
            pltpu.VMEM((nc, rows, cc), f32),
            pltpu.VMEM((nc, rows, cc), bf16),
            pltpu.VMEM((2, nc, a, rows, cc), f32),
            pltpu.VMEM((nc, a, rows, cc), f32),
            dma((3, a, b)),
            dma((2, nc, b)),
            dma((3, nc)),
            dma((nc, a)),
            dma((2, nc, a)),
            dma((2, nc, a)),
            dma((2, nc, a)),
            dma((nc, a, b)),
            dma((nc, a, b)),
            dma((nc, 2, m)),
            dma((nc, 2, m)),
            dma((nc, 3)),
        ],
        compiler_params=pltpu.CompilerParams(
            collective_id=0, has_side_effects=True, vmem_limit_bytes=60 * 1024 * 1024),
        cost_estimate=pl.CostEstimate(flops=flops, bytes_accessed=4 * dim * full, transcendentals=rows * full),
    )(patches.T, cotangent, weight, accum)


def solution(mesh):
    return jax.shard_map(
        functools.partial(shards, mesh.shape["dp"], mesh.shape["mp"]),
        mesh=mesh,
        in_specs=(P("dp", None), P("dp", "mp"), P("dp", "mp"), P("dp", "mp")),
        out_specs=(P(("dp", "mp"), None), P(("dp", "mp"), None), P(None, "mp")),
        check_vma=False,
    )
```

time: 431 us -> 246 us (0.57)
  waiting for transfers between devices: 243 us -> 0 us
  Pallas kernels: 0 us -> 228 us
  blocking collectives: 137 us -> 0 us
  between operations: 14.1 us -> 0.65 us
  matrix products: 12.9 us -> 0 us
    pallas_call x0 -> x1, Pallas kernels: none -> 228 us  [shards(): pl.pallas_call(functools.partial(kernel, a, b, m), out_shape=(jax.ShapeDt...]
    all_gather x2 -> x0, waiting for transfers between devices: 220 us -> none  [the longest x1 158 us: shards(): lax.all_gather(cotangent, 'dp', axis=0, tiled=True)]
    all_to_all x2 -> x0, blocking collectives: 137 us -> none  [the longest x1 107 us: shards(): lax.all_to_all(patches, 'dp', split_axis=1, concat_axis=0, tiled=True)]
    all_to_all x1 -> x0, waiting for transfers between devices: 22.5 us -> none  [shards(): lax.all_to_all(accum_block, 'mp', split_axis=0, concat_axis=1, tiled=True)]
    dot_general x1 -> x0, matrix products: 12.9 us -> none  [shards(): jnp.einsum('tr,tf->rf', patch_block, lax.all_gather(cotangent, 'dp', axis...]
    all_to_all x3 -> x0, local copies, waits for them, and re-layouts: 7.45 us -> none  [the longest x1 3.14 us: shards(): lax.all_to_all(weight_block, 'mp', split_axis=0, concat_axis=1, tiled=True)]
    unnamed x2 -> x6, local copies, waits for them, and re-layouts: 11.3 us -> 16.9 us
  transfers between devices with their start and end apart: 3 -> 0, of which waited for: 3 -> 0; matrix products, arithmetic and copies ran while one was open for 2% -> 0% of each run, Pallas kernels for 0% -> 0%
where the time goes in v1:
time: 246 us
  Pallas kernels  228 us (93%)
  local copies, waits for them, and re-layouts  16.9 us (7%)
    pallas_call x1, Pallas kernels, shards(): pl.pallas_call(functools.partial(kernel, a, b, m), out_shape=(jax.ShapeDt...  228 us
    unnamed x6, local copies, waits for them, and re-layouts  16.9 us

profile of v1, /device:TPU:0, one launch (start us, length us, event | category | flops | bytes accessed | tf_op | source)
XLA Modules:
  0.0 245.5 jit_solution(10974351036141904760)
XLA Ops:
  0.6 3.9 %copy.7 = bf16[512,2048]{0,1:T(8,128)(2,1)} copy(bf16[512,2048]{1,0:T(8,128)(2,1)} %param.4) | data formatting | bytes 4194304 | tf_op args[0]
  4.6 228.0 %shard_map.67 = (f32[64,8192]{1,0:T(8,128)}, f32[64,8192]{1,0:T(8,128)}, bf16[2048,2048]{1,0:T(8,128)(2,1)}) custom-call(bf16[2048,512]{1,0:T(8,128)(2,1)} %bitcast.1, bf16[512,2048]{1,0:T(8,128)(2,1)} %t_ref.1, f32[256,2048]{1,0:T(8,128)} %w_ref.1, f32[256,2048]{1,0:T(8,128)} %s_ref.1), custom_call_target="tpu_custom_call" | custom-call | flops 4294967296 | bytes 16777216 | tf_op jit(solution)/shard_map/pallas_call | solution.py:265
  232.5 0.0 copy-start
  232.5 3.2 %copy.11 = f32[64,8192]{1,0:T(8,128)} copy(f32[64,8192]{1,0:T(8,128)} %get-tuple-element.6) | data formatting | bytes 4194304
  235.8 0.0 copy-done
  235.8 1.3 copy.12
  237.1 8.4 %copy.13 = bf16[2048,2048]{1,0:T(8,128)(2,1)} copy(bf16[2048,2048]{1,0:T(8,128)(2,1)} %get-tuple-element.8) | data formatting | bytes 16777216
Async XLA Ops:
  232.5 3.2 %copy-start = (f32[64,8192]{1,0:T(8,128)S(1)}, f32[64,8192]{1,0:T(8,128)}, u32[]{:S(2)}) copy-start(f32[64,8192]{1,0:T(8,128)} %get-tuple-element.7) | copy-start | bytes 6291460

commit v2 on v1

--- a/solution.py
+++ b/solution.py
@@ -11,7 +11,7 @@
 chunks = 8
 
 
-def kernel(a, b, m, p_ref, t_ref, w_ref, s_ref, ow_ref, os_ref, oc_ref,
+def kernel(a, b, m, direct, p_ref, t_ref, w_ref, s_ref, ow_ref, os_ref, oc_ref,
            pv, tv, wv, sv, cv, rbuf, sbuf,
            psem, tsem, lsem, rsend, rrecv, csend, crecv, xsend, xrecv, msend, mrecv, osem):
     nc, _, tok, cc = tv.shape
@@ -46,6 +46,9 @@
     def block(i):
         return pl.ds(pl.multiple_of(i * rows, rows), rows)
 
+    def features(i):
+        return p_ref.at[:, block(i)] if direct else p_ref.at[block(i)]
+
     def own_tokens(c):
         return pltpu.make_async_copy(t_ref.at[:, cols(c)], tv.at[c, xi], lsem.at[0, c])
 
@@ -56,7 +59,7 @@
         return pltpu.make_async_copy(s_ref.at[:, cols(c)], sv.at[c], lsem.at[2, c])
 
     def own_features(d):
-        return pltpu.make_async_copy(p_ref.at[block(d * b + xi)], pv.at[d, xi], psem.at[2, d, 0])
+        return pltpu.make_async_copy(features(d * b + xi), pv.at[d, xi], psem.at[2, d, 0])
 
     def send_tokens(c, j):
         return remote(t_ref.at[:, cols(c)], tv.at[c, xi], tsem.at[0, c, j], tsem.at[1, c, j], peer(j))
@@ -65,10 +68,10 @@
         return remote(t_ref.at[:, cols(c)], tv.at[c, inner(b - j)], tsem.at[0, c, j], tsem.at[1, c, j], peer(j))
 
     def send_features(d, j):
-        return remote(p_ref.at[block(d * b + inner(j))], pv.at[d, xi], psem.at[0, d, j], psem.at[1, d, j], peer(j))
+        return remote(features(d * b + inner(j)), pv.at[d, xi], psem.at[0, d, j], psem.at[1, d, j], peer(j))
 
     def recv_features(d, j):
-        return remote(p_ref.at[block(d * b + xi)], pv.at[d, inner(b - j)], psem.at[0, d, j], psem.at[1, d, j], peer(j))
+        return remote(features(d * b + xi), pv.at[d, inner(b - j)], psem.at[0, d, j], psem.at[1, d, j], peer(j))
 
     def pass_sum(side, c, d):
         return remote(sbuf.at[c, d], rbuf.at[side, c, d], rsend.at[c, d], rrecv.at[side, c, d],
@@ -135,39 +138,44 @@
 
     for j in range(1, b):
         send_tokens(0, j).start()
-    order = []
-    for k in range(a):
-        for d in (a - 1 - k, k):
-            if d not in order:
-                order.append(d)
-    for d in order:
+    def in_order(do):
+        for k in range(a):
+            pl.when(a - 1 - k > zi)(functools.partial(do, 0, a - 1 - k))
+            pl.when(k < zi)(functools.partial(do, 1, k))
+
+    def start_features(_, d):
         for j in range(1, b):
             send_features(d, j).start()
+
+    in_order(start_features)
+    start_features(0, zi)
 
     @pl.loop(1, nc)
     def _(c):
         for j in range(1, b):
             send_tokens(c, j).start()
 
+    def product(p, t):
+        return lax.dot_general(p, t, (((0 if direct else 1,), (0,)), ((), ())), preferred_element_type=jnp.float32)
+
     def partial(c, d):
-        total = jnp.dot(pv[d, 0], tv[c, 0], preferred_element_type=jnp.float32)
+        total = product(pv[d, 0], tv[c, 0])
         for x in range(1, b):
-            total += jnp.dot(pv[d, x], tv[c, x], preferred_element_type=jnp.float32)
+            total += product(pv[d, x], tv[c, x])
         return total
+
+    def features_here(d):
+        own_features(d).wait()
+        for j in range(1, b):
+            recv_features(d, j).wait_recv()
 
     def stage_sums(c):
         own_tokens(c).wait()
         for j in range(1, b):
             recv_tokens(c, j).wait_recv()
 
-        @pl.when(c == 0)
-        def _():
-            for d in order:
-                own_features(d).wait()
-                for j in range(1, b):
-                    recv_features(d, j).wait_recv()
-
         def step(side, d):
+            pl.when(c == 0)(lambda: features_here(d))
             sbuf[c, d] = partial(c, d)
 
             @pl.when(has_left if side == 0 else has_right)
@@ -177,11 +185,10 @@
 
             pass_sum(side, c, d).start()
 
-        for k in range(a):
-            pl.when(a - 1 - k > zi)(functools.partial(step, 0, a - 1 - k))
-            pl.when(k < zi)(functools.partial(step, 1, k))
+        in_order(step)
 
     def stage_update(c):
+        pl.when(c == 0)(lambda: features_here(zi))
         own_weight(c).wait()
         own_accum(c).wait()
         sbuf[c, zi] = partial(c, zi)
@@ -256,6 +263,7 @@
         a *= 2
     b = n // a
     nc = chunks
+    direct = weight.shape[0] % 128 == 0
     tok, dim = patches.shape
     rows, full = weight.shape
     cc = full // nc
@@ -263,16 +271,16 @@
     dma = pltpu.SemaphoreType.DMA
     flops = 2 * tok * b * a * rows * full
     return pl.pallas_call(
-        functools.partial(kernel, a, b, m),
+        functools.partial(kernel, a, b, m, direct),
         out_shape=(
-            jax.ShapeDtypeStruct((rows // m, full * m), f32),
-            jax.ShapeDtypeStruct((rows // m, full * m), f32),
-            jax.ShapeDtypeStruct((dim, full), bf16),
+            pltpu.VMEM((rows // m, full * m), f32),
+            pltpu.VMEM((rows // m, full * m), f32),
+            pltpu.VMEM((dim, full), bf16),
         ),
         in_specs=[pl.BlockSpec(memory_space=pl.ANY)] * 4,
-        out_specs=(pl.BlockSpec(memory_space=pl.ANY),) * 3,
+        out_specs=(pl.BlockSpec(memory_space=pltpu.VMEM),) * 3,
         scratch_shapes=[
-            pltpu.VMEM((a, b, rows, tok), bf16),
+            pltpu.VMEM((a, b, tok, rows) if direct else (a, b, rows, tok), bf16),
             pltpu.VMEM((nc, b, tok, cc), bf16),
             pltpu.VMEM((nc, rows, cc), f32),
             pltpu.VMEM((nc, rows, cc), f32),
@@ -293,9 +301,9 @@
             dma((nc, 3)),
         ],
         compiler_params=pltpu.CompilerParams(
-            collective_id=0, has_side_effects=True, vmem_limit_bytes=60 * 1024 * 1024),
+            collective_id=0, has_side_effects=True, vmem_limit_bytes=42 * 1024 * 1024),
         cost_estimate=pl.CostEstimate(flops=flops, bytes_accessed=4 * dim * full, transcendentals=rows * full),
-    )(patches.T, cotangent, weight, accum)
+    )(patches if direct else patches.T, cotangent, weight, accum)
 
 
 def solution(mesh):

time: 246 us -> 224 us (0.911)
  Pallas kernels: 228 us -> 217 us
  local copies, waits for them, and re-layouts: 16.9 us -> 6.04 us
    unnamed x6 -> x3, local copies, waits for them, and re-layouts: 16.9 us -> 6.04 us
    pallas_call x1, Pallas kernels: 228 us -> 217 us  [shards(): pl.pallas_call(functools.partial(kernel, a, b, m, direct), out_shape=(plt...]
where the time goes in v2:
time: 224 us
  Pallas kernels  217 us (97%)
  local copies, waits for them, and re-layouts  6.04 us (3%)
    pallas_call x1, Pallas kernels, shards(): pl.pallas_call(functools.partial(kernel, a, b, m, direct), out_shape=(plt...  217 us
    unnamed x3, local copies, waits for them, and re-layouts  6.04 us

profile of v2, /device:TPU:0, one launch (start us, length us, event | category | flops | bytes accessed | tf_op | source)
XLA Modules:
  0.0 223.8 jit_solution(7927745257077757391)
XLA Ops:
  0.6 217.2 %shard_map.67 = (f32[64,8192]{1,0:T(8,128)S(1)}, f32[64,8192]{1,0:T(8,128)S(1)}, bf16[2048,2048]{1,0:T(8,128)(2,1)S(1)}) custom-call(bf16[512,2048]{1,0:T(8,128)(2,1)} %p_ref.1, bf16[512,2048]{1,0:T(8,128)(2,1)} %t_ref.1, f32[256,2048]{1,0:T(8,128)} %w_ref.1, f32[256,2048]{1,0:T(8,128)} %s_ref.1), custom_call_target="tpu_custom_call" | custom-call | flops 4294967296 | bytes 16777216 | tf_op jit(solution)/shard_map/pallas_call | solution.py:273
  217.8 1.3 copy.10
  219.1 1.3 copy.11
  220.4 3.4 %copy.12 = bf16[2048,2048]{1,0:T(8,128)(2,1)} copy(bf16[2048,2048]{1,0:T(8,128)(2,1)S(1)} %get-tuple-element.5) | data formatting | bytes 16777216
